TPU v7x, 16 devices: a whole 2x2x2 slice. The times are simulated.
16 devices in a mesh: data: 4 (over z, y), tp: 4 (over x, core).
Axes of the slice: x: 2, y: 2, z: 2, core: 2. Of those that a mesh axis runs over, the one named last changes fastest.
Arguments:
- x_in: bfloat16 [16384, 4096], P('data'), parts along dimension 0
- w_gate: bfloat16 [4096, 14336], P(None, 'tp')
- w_up: bfloat16 [4096, 14336], P(None, 'tp')
- w_down: bfloat16 [14336, 4096], P('tp')
- residual: bfloat16 [16384, 4096], P(('data', 'tp')), parts along dimension 0
- norm_gain: float32 [4096], replicated
Outputs:
- output 1: bfloat16 [16384, 4096], P(('data', 'tp')), parts along dimension 0
- output 2: bfloat16 [16384, 4096], P(('data', 'tp')), parts along dimension 0
There are 4 independent parts. A program takes and returns all parts, laid end to end along the dimension named above; an argument that names none is the same for every part.
All inputs are finite; a program needn't handle non-finite values.
Results may differ from a plain program's by a relative error of at most 0.00659775.
Values are sent between devices in bfloat16 or wider.
A program may use at most 1 GiB of HBM per device.

v0:
```python
import jax
import jax.numpy as jnp
from jax import lax
from jax.sharding import PartitionSpec as P

EPS = 1e-5


def add_and_norm(y_sum, residual, norm_gain):
    hidden_sum = residual.astype(jnp.float32) + y_sum
    mean_sq = jnp.mean(hidden_sum * hidden_sum, axis=-1, keepdims=True)
    normed = hidden_sum * lax.rsqrt(mean_sq + EPS) * norm_gain
    return hidden_sum.astype(jnp.bfloat16), normed.astype(jnp.bfloat16)


def solution(mesh):
    tp_size = mesh.shape["tp"]

    def local_block(x_in, w_gate, w_up, w_down, residual, norm_gain):
        gate_val = jnp.dot(x_in, w_gate, preferred_element_type=jnp.float32)
        up_val = jnp.dot(x_in, w_up, preferred_element_type=jnp.float32)
        hidden = (jax.nn.silu(gate_val) * up_val).astype(jnp.bfloat16)
        part_prod = jnp.dot(hidden, w_down, preferred_element_type=jnp.float32).astype(jnp.bfloat16)
        received = lax.all_to_all(part_prod, "tp", 0, 0, tiled=True)
        rows = residual.shape[0]
        y_sum = jnp.sum(received.reshape(tp_size, rows, received.shape[1]), axis=0, dtype=jnp.float32)
        return add_and_norm(y_sum, residual, norm_gain)

    row_spec = P(("data", "tp"), None)
    return jax.shard_map(local_block, mesh=mesh, in_specs=(P("data", None), P(None, "tp"), P(None, "tp"), P("tp", None), row_spec, P(None)), out_specs=(row_spec, row_spec), check_vma=False)
```

profile of v0, /device:TPU:0, one launch (start us, length us, event | category | flops | bytes accessed | tf_op | source)
XLA Modules:
  0.0 812.4 jit_solution(4379627099762553088)
XLA Ops:
  0.6 134.1 %fusion.1 = f32[4096,3584]{1,0:T(8,128)} fusion(bf16[4096,4096]{1,0:T(8,128)(2,1)} %param.6, bf16[4096,3584]{1,0:T(8,128)(2,1)} %param.7), kind=kOutput, calls=%fused_computation.8 | convolution fusion | flops 120259084288 | bytes 121634816 | tf_op jit(solution)/shard_map/dot_general | solution.py:20
  134.7 134.7 %multiply_convert_fusion = bf16[4096,3584]{1,0:T(8,128)(2,1)} fusion(f32[4096,3584]{1,0:T(8,128)} %fusion.1, bf16[4096,4096]{1,0:T(8,128)(2,1)} %param.6, bf16[4096,3584]{1,0:T(8,128)(2,1)} %param.8), kind=kOutput, calls=%fused_computation.1 | convolution fusion | flops 120347164672 | bytes 150994944 | tf_op jit(solution)/shard_map/dot_general | solution.py:21
  269.4 132.1 %convolution_convert_fusion = bf16[4096,4096]{1,0:T(8,128)(2,1)} fusion(bf16[4096,3584]{1,0:T(8,128)(2,1)} %multiply_convert_fusion, bf16[3584,4096]{1,0:T(8,128)(2,1)} %param.9), kind=kOutput, calls=%fused_computation.2 | convolution fusion | flops 120275861504 | bytes 92274688 | tf_op jit(solution)/shard_map/dot_general | solution.py:23
  401.5 381.6 %all_to_all.9 = bf16[4,1024,4096]{2,1,0:T(8,128)(2,1)} all-to-all(bf16[4,1024,4096]{2,1,0:T(8,128)(2,1)} %bitcast.7), channel_id=1, replica_groups=mesh['data'=4,'tp'=4] {'tp'}, dimensions={0} | all-to-all | bytes 67108864 | tf_op jit(solution)/shard_map/all_to_all | solution.py:24
  783.0 0.0 copy-start
  783.0 0.0 copy-start.1
  783.0 19.0 %convert_reduce_fusion = f32[1024,4096]{1,0:T(8,128)S(1)} fusion(bf16[4,1024,4096]{2,1,0:T(8,128)(2,1)} %all_to_all.9), kind=kLoop, calls=%fused_computation | loop fusion | flops 29360128 | bytes 50331648 | tf_op jit(solution)/shard_map/reduce_sum | solution.py:26
  802.1 0.0 copy-done
  802.1 2.5 multiply_reduce_fusion
  804.6 0.0 copy-done.1
  804.6 7.7 multiply_convert_fusion.1
  (1 shorter events, 0.0 us)
Async XLA Ops:
  783.0 19.0 %copy-start = (bf16[1024,4096]{1,0:T(8,128)(2,1)S(1)}, bf16[1024,4096]{1,0:T(8,128)(2,1)}, u32[]{:S(2)}) copy-start(bf16[1024,4096]{1,0:T(8,128)(2,1)} %param.10) | copy-start | bytes 25165828
  783.0 21.6 %copy-start.1 = (f32[4096]{0:T(1024)S(1)}, f32[4096]{0:T(1024)}, u32[]{:S(2)}) copy-start(f32[4096]{0:T(1024)} %param.11) | copy-start | bytes 49156
where the time goes:
time: 813 us; the launch traced here: 812 us
  matrix products  401 us (49%)
  blocking collectives  382 us (47%)
  other arithmetic  29.3 us (4%)
    all_to_all x1, blocking collectives, local_block(): received = lax.all_to_all(part_prod, 'tp', 0, 0, tiled=True)  382 us
    dot_general x1, matrix products, local_block(): up_val = jnp.dot(x_in, w_up, preferred_element_type=jnp.float32)  135 us
    dot_general x1, matrix products, local_block(): gate_val = jnp.dot(x_in, w_gate, preferred_element_type=jnp.float32)  134 us
    dot_general x1, matrix products, local_block(): jnp.dot(hidden, w_down, preferred_element_type=jnp.float32)  132 us
    reduce_sum x1, other arithmetic, local_block(): jnp.sum(received.reshape(tp_size, rows, received.shape[1]), axis=0, dtype...  19 us

commit v1 on v0

v1 whole, which is shorter than its diff:
```python
import functools

import jax
import jax.numpy as jnp
from jax import lax
from jax.experimental import pallas as pl
from jax.experimental.pallas import tpu as pltpu
from jax.sharding import PartitionSpec as P

EPS = 1e-5
TP = 4
M = 512
NG = 512
ND = 512
SUB = 256
FB = 64
ROWS = 16
TAIL = 4

bf16 = jnp.bfloat16
f32 = jnp.float32


def kernel(x_hbm, wg_hbm, wu_hbm, wd_hbm, res_hbm, gain_ref,
           h_hbm, n_hbm, y_hbm, r_hbm,
           x_v, wg_v, wu_v, wd_v, g_v, y_v, in_v, out_v,
           x_sem, wg_sem, wu_sem, wd_sem, y_sem, in_sem, out_sem,
           send_sem, recv_sem, tsend_sem, trecv_sem):
    D, FS = wg_hbm.shape
    R = res_hbm.shape[0]
    HALVES = R // M
    assert HALVES == 2
    n_gu, n_dn = FS // NG, D // ND
    n_chunk = TP * HALVES
    me = lax.axis_index("tp")
    far_same = lax.rem(me + 2, TP)
    far_other = TP - 1 - me
    near = me + 1 - 2 * lax.rem(me, 2)
    peers = (far_same, far_other, near)

    barrier = pltpu.get_barrier_semaphore()
    for peer in peers:
        pl.semaphore_signal(barrier, inc=1, device_id={"tp": peer}, device_id_type=pl.DeviceIdType.MESH)
    pl.semaphore_wait(barrier, TP - 1)

    def slot_of(c):
        late = c // 4
        return (1 - late) * lax.rem(c, 2) + late * (2 + (c - 4) // 2)

    def half_of(c):
        late = c // 4
        return (1 - late) * (c // 2) + late * lax.rem(c, 2)

    def owner_of(c):
        late = c // 4
        odd = lax.rem(c, 2)
        far = (1 - odd) * far_same + odd * far_other
        own = (c - 4) // 2
        close = (1 - own) * near + own * me
        return (1 - late) * far + late * close

    def x_copy(c):
        row = pl.multiple_of(owner_of(c) * R + half_of(c) * M, M)
        return pltpu.make_async_copy(x_hbm.at[pl.ds(row, M), :], x_v, x_sem)

    def gu_copies(j, s):
        col = pl.multiple_of(j * NG, NG)
        return (pltpu.make_async_copy(wg_hbm.at[:, pl.ds(col, NG)], wg_v.at[s], wg_sem.at[s]),
                pltpu.make_async_copy(wu_hbm.at[:, pl.ds(col, NG)], wu_v.at[s], wu_sem.at[s]))

    def wd_copy(d, s):
        col = pl.multiple_of(d * ND, ND)
        return pltpu.make_async_copy(wd_hbm.at[:, pl.ds(col, ND)], wd_v.at[s], wd_sem.at[s])

    def y_copy(c, d):
        row = pl.multiple_of(half_of(c) * M, M)
        col = pl.multiple_of(d * ND, ND)
        s = lax.rem(d, 2)
        return pltpu.make_async_copy(y_v.at[s], y_hbm.at[slot_of(c), pl.ds(row, M), pl.ds(col, ND)], y_sem.at[s])

    def remote(slot, row, rows, cols, ssem, rsem):
        ref = (slot, pl.ds(row, rows)) + ((cols,) if cols is not None else (slice(None),))
        return pltpu.make_async_remote_copy(
            src_ref=y_hbm.at[ref], dst_ref=r_hbm.at[ref], send_sem=ssem, recv_sem=rsem,
            device_id={"tp": peers[slot]}, device_id_type=pl.DeviceIdType.MESH)

    def chunk_copy(c):
        slot = (0, 1, 0, 1, 2, 2)[c]
        half = (0, 0, 1, 1, 0, 1)[c]
        return remote(slot, half * M, M, None, send_sem.at[c], recv_sem.at[c])

    def first_piece(d):
        col = pl.multiple_of(d * ND, ND)
        return remote(0, 0, M, pl.ds(col, ND), send_sem.at[0], recv_sem.at[0])

    def tail_piece(t):
        rows = M // TAIL
        return remote(1, M + t * rows, rows, None, tsend_sem.at[t], trecv_sem.at[t])

    def send_chunk(c):
        if c == 3:
            for t in range(TAIL):
                tail_piece(t).start()
        else:
            chunk_copy(c).start()

    x_copy(0).start()
    for cp in gu_copies(0, 0):
        cp.start()

    def chunk(c, _):
        x_copy(c).wait()

        def gu_step(j, _):
            g = c * n_gu + j
            s = lax.rem(g, 2)

            @pl.when(j + 1 < n_gu)
            def _():
                for cp in gu_copies(j + 1, 1 - s):
                    cp.start()

            @pl.when(j == n_gu - 3)
            def _():
                wd_copy(0, 0).start()

            @pl.when(j == n_gu - 2)
            def _():
                wd_copy(1, 1).start()

            for cp in gu_copies(j, s):
                cp.wait()
            for q in range(NG // SUB):
                cols = slice(q * SUB, (q + 1) * SUB)
                gate = jnp.dot(x_v[...], wg_v[s, :, cols], preferred_element_type=f32)
                up = jnp.dot(x_v[...], wu_v[s, :, cols], preferred_element_type=f32)
                hid = (gate * jax.nn.sigmoid(gate) * up).astype(bf16)
                g_v[:, pl.ds(pl.multiple_of(j * NG + q * SUB, SUB), SUB)] = hid
            return 0

        lax.fori_loop(0, n_gu, gu_step, 0)

        def dn_step(d, _):
            @pl.when(d + 2 < n_dn)
            def _():
                wd_copy(d + 2, lax.rem(d + 2, 3)).start()

            @pl.when((d == 2) & (c + 1 < n_chunk))
            def _():
                x_copy(c + 1).start()

            @pl.when((d == 4) & (c + 1 < n_chunk))
            def _():
                for cp in gu_copies(0, lax.rem((c + 1) * n_gu, 2)):
                    cp.start()

            wd_copy(d, lax.rem(d, 3)).wait()

            @pl.when(d >= 1)
            def _():
                y_copy(c, d - 1).wait()

            @pl.when((d >= 1) & (c == 0))
            def _():
                first_piece(d - 1).start()

            y = jnp.dot(g_v[...], wd_v[lax.rem(d, 3)], preferred_element_type=f32)
            y_v[lax.rem(d, 2)] = y.astype(bf16)
            y_copy(c, d).start()
            return 0

        lax.fori_loop(0, n_dn, dn_step, 0)
        y_copy(c, n_dn - 1).wait()

        @pl.when(c == 0)
        def _():
            first_piece(n_dn - 1).start()

        for k in range(1, 6):
            @pl.when(c == k)
            def _(k=k):
                send_chunk(k)
        return 0

    lax.fori_loop(0, n_chunk, chunk, 0)

    def in_copies(b, s):
        row = pl.multiple_of(b * FB, FB)
        out = [pltpu.make_async_copy(res_hbm.at[pl.ds(row, FB), :], in_v.at[s, 0], in_sem.at[s, 0]),
               pltpu.make_async_copy(y_hbm.at[3, pl.ds(row, FB), :], in_v.at[s, 1], in_sem.at[s, 1])]
        for k in range(3):
            out.append(pltpu.make_async_copy(r_hbm.at[k, pl.ds(row, FB), :], in_v.at[s, 2 + k], in_sem.at[s, 2 + k]))
        return out

    def out_copies(b, s):
        row = pl.multiple_of(b * FB, FB)
        return (pltpu.make_async_copy(out_v.at[s, 0], h_hbm.at[pl.ds(row, FB), :], out_sem.at[s, 0]),
                pltpu.make_async_copy(out_v.at[s, 1], n_hbm.at[pl.ds(row, FB), :], out_sem.at[s, 1]))

    n_fb = R // FB
    per_tail = M // TAIL // FB

    def need(b):
        @pl.when(b == n_fb // 2)
        def _():
            for c in (2, 5):
                chunk_copy(c).wait_recv()
        for t in range(TAIL):
            @pl.when(b == n_fb // 2 + t * per_tail)
            def _(t=t):
                tail_piece(t).wait_recv()

    for c in (0, 1, 4):
        chunk_copy(c).wait_recv()
    for cp in in_copies(0, 0):
        cp.start()

    def final(b, _):
        s = lax.rem(b, 2)
        need(b + 1)

        @pl.when(b + 1 < n_fb)
        def _():
            for cp in in_copies(b + 1, 1 - s):
                cp.start()

        for cp in in_copies(b, s):
            cp.wait()

        @pl.when(b >= 2)
        def _():
            for cp in out_copies(b - 2, s):
                cp.wait()

        def rows_step(i, _):
            rows = pl.ds(pl.multiple_of(i * ROWS, ROWS), ROWS)
            h = in_v[s, 0, rows, :].astype(f32)
            y = in_v[s, 1, rows, :].astype(f32)
            for k in range(3):
                y = y + in_v[s, 2 + k, rows, :].astype(f32)
            h = h + y
            mean_sq = jnp.mean(h * h, axis=-1, keepdims=True)
            out_v[s, 0, rows, :] = h.astype(bf16)
            out_v[s, 1, rows, :] = (h * lax.rsqrt(mean_sq + EPS) * gain_ref[...]).astype(bf16)
            return 0

        lax.fori_loop(0, FB // ROWS, rows_step, 0)
        for cp in out_copies(b, s):
            cp.start()
        return 0

    lax.fori_loop(0, n_fb, final, 0)
    for b in (n_fb - 2, n_fb - 1):
        for cp in out_copies(b, b % 2):
            cp.wait()
    for c in (0, 1, 2, 4, 5):
        chunk_copy(c).wait_send()
    for t in range(TAIL):
        tail_piece(t).wait_send()


def solution(mesh):
    def local_block(x_in, w_gate, w_up, w_down, residual, norm_gain):
        T, D = x_in.shape
        FS = w_gate.shape[1]
        R = residual.shape[0]
        any_ = pl.BlockSpec(memory_space=pl.ANY)
        h_out, n, _, _ = pl.pallas_call(
            kernel,
            out_shape=(jax.ShapeDtypeStruct((R, D), bf16), jax.ShapeDtypeStruct((R, D), bf16),
                       jax.ShapeDtypeStruct((TP, R, D), bf16), jax.ShapeDtypeStruct((TP - 1, R, D), bf16)),
            in_specs=[any_] * 5 + [pl.BlockSpec(memory_space=pltpu.VMEM)],
            out_specs=(any_,) * 4,
            scratch_shapes=[
                pltpu.VMEM((M, D), bf16),
                pltpu.VMEM((2, D, NG), bf16),
                pltpu.VMEM((2, D, NG), bf16),
                pltpu.VMEM((3, FS, ND), bf16),
                pltpu.VMEM((M, FS), bf16),
                pltpu.VMEM((2, M, ND), bf16),
                pltpu.VMEM((2, 5, FB, D), bf16),
                pltpu.VMEM((2, 2, FB, D), bf16),
                pltpu.SemaphoreType.DMA,
                pltpu.SemaphoreType.DMA((2,)),
                pltpu.SemaphoreType.DMA((2,)),
                pltpu.SemaphoreType.DMA((3,)),
                pltpu.SemaphoreType.DMA((2,)),
                pltpu.SemaphoreType.DMA((2, 5)),
                pltpu.SemaphoreType.DMA((2, 2)),
                pltpu.SemaphoreType.DMA((6,)),
                pltpu.SemaphoreType.DMA((6,)),
                pltpu.SemaphoreType.DMA((TAIL,)),
                pltpu.SemaphoreType.DMA((TAIL,)),
            ],
            compiler_params=pltpu.CompilerParams(collective_id=0, has_side_effects=True, vmem_limit_bytes=60 * 1024 * 1024),
            name="mlp_block",
        )(x_in, w_gate, w_up, w_down, residual, norm_gain.reshape(1, D))
        return h_out, n

    row_spec = P(("data", "tp"), None)
    return jax.shard_map(local_block, mesh=mesh, in_specs=(P("data", None), P(None, "tp"), P(None, "tp"), P("tp", None), row_spec, P(None)), out_specs=(row_spec, row_spec), check_vma=False)
```

time: 813 us -> 492 us (0.61)
  Pallas kernels: 0 us -> 475 us
  matrix products: 401 us -> 0 us
  blocking collectives: 382 us -> 0 us
  other arithmetic: 29.3 us -> 0 us
  local copies, waits for them, and re-layouts: 0.01 us -> 15.8 us
    pallas_call x0 -> x1, Pallas kernels: none -> 475 us  [local_block(): pl.pallas_call(kernel, out_shape=(jax.ShapeDtypeStruct((R, D), bf16), jax...]
    dot_general x3 -> x0, matrix products: 401 us -> none  [the longest x1 135 us: local_block(): up_val = jnp.dot(x_in, w_up, preferred_element_type=jnp.float32)]
    all_to_all x1 -> x0, blocking collectives: 382 us -> none  [local_block(): received = lax.all_to_all(part_prod, 'tp', 0, 0, tiled=True)]
    reduce_sum x2 -> x0, other arithmetic: 21.5 us -> none  [the longest x1 19 us: local_block(): jnp.sum(received.reshape(tp_size, rows, received.shape[1]), axis=0, dtype...]
    unnamed x4 -> x2, local copies, waits for them, and re-layouts: 0.01 us -> 15.8 us
where the time goes in v1:
time: 492 us; the launch traced here: 491 us
  Pallas kernels  475 us (97%)
  local copies, waits for them, and re-layouts  15.8 us (3%)
    pallas_call x1, Pallas kernels, local_block(): pl.pallas_call(kernel, out_shape=(jax.ShapeDtypeStruct((R, D), bf16), jax...  475 us
    unnamed x2, local copies, waits for them, and re-layouts  15.8 us

profile of v1, /device:TPU:0, one launch (start us, length us, event | category | flops | bytes accessed | tf_op | source)
XLA Modules:
  0.0 491.1 jit_solution(1987965276726890117)
XLA Ops:
  0.6 474.7 %mlp_block.1 = (bf16[1024,4096]{1,0:T(8,128)(2,1)}, bf16[1024,4096]{1,0:T(8,128)(2,1)}, bf16[4,1024,4096]{2,1,0:T(8,128)(2,1)}, bf16[3,1024,4096]{2,1,0:T(8,128)(2,1)}) custom-call(bf16[4096,4096]{1,0:T(8,128)(2,1)} %x_hbm.1, bf16[4096,3584]{1,0:T(8,128)(2,1)} %wg_hbm.1, bf16[4096,3584]{1,0:T(8,128)(2,1)} %wu_hbm.1, bf16[3584,4096]{1,0:T(8,128)(2,1)} %wd_hbm.1, ...), custom_call_target="tpu_custom_call" | custom-call | tf_op jit(solution)/shard_map/mlp_block/pallas_call | solution.py:268
  475.3 7.9 %copy.10 = bf16[1024,4096]{1,0:T(8,128)(2,1)} copy(bf16[1024,4096]{1,0:T(8,128)(2,1)} %get-tuple-element.8) | data formatting | bytes 16777216
  483.2 7.9 %copy.11 = bf16[1024,4096]{1,0:T(8,128)(2,1)} copy(bf16[1024,4096]{1,0:T(8,128)(2,1)} %get-tuple-element.9) | data formatting | bytes 16777216

commit v2 on v0

v2 whole, which is shorter than its diff:
```python
import jax
import jax.numpy as jnp
from jax import lax
from jax.experimental import pallas as pl
from jax.experimental.pallas import tpu as pltpu
from jax.sharding import PartitionSpec as P

EPS = 1e-5
TP = 4
M = 512
SUB = 256
ND = 512
BIG = 1024
TAIL = 4
FB = 256
ROWS = 8

bf16 = jnp.bfloat16
f32 = jnp.float32


def matmul_kernel(x_hbm, wg_hbm, wu_hbm, wd_hbm, y_hbm, r_hbm,
                  x_v, wg_v, wu_v, wd_v, g_v, y_v,
                  x_sem, wg_sem, wu_sem, wd_sem, y_sem, send_sem, recv_sem):
    D, FS = wg_hbm.shape
    R = y_hbm.shape[1]
    assert R == 2 * M and R == BIG
    n_gu, n_dn = FS // (2 * SUB), D // ND
    me = lax.axis_index("tp")
    far_same = lax.rem(me + 2, TP)
    far_other = TP - 1 - me
    near = me + 1 - 2 * lax.rem(me, 2)
    peers = (far_same, far_other, near)

    barrier = pltpu.get_barrier_semaphore()
    for peer in peers:
        pl.semaphore_signal(barrier, inc=1, device_id={"tp": peer}, device_id_type=pl.DeviceIdType.MESH)
    pl.semaphore_wait(barrier, TP - 1)

    def owner_of(c):
        own = c // 2
        mid = (1 - own) * ((1 - c) * far_other + c * near)
        return mid + own * me

    def x_small(c):
        row = pl.multiple_of(far_same * R + c * M, M)
        return pltpu.make_async_copy(x_hbm.at[pl.ds(row, M), :], x_v.at[pl.ds(0, M), :], x_sem)

    def x_big(c):
        row = pl.multiple_of(owner_of(c) * R, BIG)
        return pltpu.make_async_copy(x_hbm.at[pl.ds(row, BIG), :], x_v, x_sem)

    def gu_copies(j, slot):
        col = pl.ds(pl.multiple_of(j * 2 * SUB, 2 * SUB), 2 * SUB)
        return (pltpu.make_async_copy(wg_hbm.at[:, col], wg_v.at[slot], wg_sem.at[slot]),
                pltpu.make_async_copy(wu_hbm.at[:, col], wu_v.at[slot], wu_sem.at[slot]))

    def dn_copy(d):
        k = lax.rem(d, 4)
        at = pl.ds(pl.multiple_of(lax.rem(k, 2) * ND, ND), ND)
        return pltpu.make_async_copy(wd_hbm.at[:, pl.ds(pl.multiple_of(d * ND, ND), ND)], wd_v.at[k // 2, :, at], wd_sem.at[k])

    def dn_big(d):
        k = lax.rem(d, 2)
        return pltpu.make_async_copy(wd_hbm.at[:, pl.ds(pl.multiple_of(d * BIG, BIG), BIG)], wd_v.at[k], wd_sem.at[k])

    def y_small(c, d):
        k = lax.rem(d, 2)
        return pltpu.make_async_copy(
            y_v.at[k, pl.ds(0, M), pl.ds(0, ND)],
            y_hbm.at[0, pl.ds(pl.multiple_of(c * M, M), M), pl.ds(pl.multiple_of(d * ND, ND), ND)], y_sem.at[k])

    def y_big(c, d):
        k = lax.rem(d, 2)
        return pltpu.make_async_copy(y_v.at[k], y_hbm.at[c + 1, :, pl.ds(pl.multiple_of(d * BIG, BIG), BIG)], y_sem.at[k])

    def remote(slot, row, rows, cols, ssem, rsem):
        ref = (slot, pl.ds(row, rows), slice(None) if cols is None else cols)
        return pltpu.make_async_remote_copy(
            src_ref=y_hbm.at[ref], dst_ref=r_hbm.at[ref], send_sem=ssem, recv_sem=rsem,
            device_id={"tp": peers[slot]}, device_id_type=pl.DeviceIdType.MESH)

    def first_piece(d):
        return remote(0, 0, M, pl.ds(pl.multiple_of(d * ND, ND), ND), send_sem.at[0], recv_sem.at[0])

    rows = R // TAIL
    copies = [remote(0, M, M, None, send_sem.at[1], recv_sem.at[1])]
    copies += [remote(1, t * rows, rows, None, send_sem.at[2 + t], recv_sem.at[2 + t]) for t in range(TAIL)]
    copies += [remote(2, 0, R, None, send_sem.at[2 + TAIL], recv_sem.at[2 + TAIL])]
    first_whole = remote(0, 0, M, None, send_sem.at[0], recv_sem.at[0])

    def hidden(m, slot, j):
        for q in range(2):
            cols = slice(q * SUB, (q + 1) * SUB)
            for r in range(m // M):
                part = slice(r * M, (r + 1) * M)
                gate = jnp.dot(x_v[part, :], wg_v[slot, :, cols], preferred_element_type=f32)
                up = jnp.dot(x_v[part, :], wu_v[slot, :, cols], preferred_element_type=f32)
                g_v[part, pl.ds(pl.multiple_of(j * 2 * SUB + q * SUB, SUB), SUB)] = (gate * jax.nn.sigmoid(gate) * up).astype(bf16)

    def gate_up(m, base, before):
        def gu_step(j, _):
            slot = lax.rem(base + j, 2)

            @pl.when(j + 1 < n_gu)
            def _():
                for cp in gu_copies(j + 1, 1 - slot):
                    cp.start()

            before(j)
            for cp in gu_copies(j, slot):
                cp.wait()
            hidden(m, slot, j)
            return 0

        lax.fori_loop(0, n_gu, gu_step, 0)

    def small_chunk(c, _):
        x_small(c).wait()

        def before(j):
            @pl.when(j >= n_gu - 3)
            def _():
                dn_copy(j - (n_gu - 3)).start()

        gate_up(M, c * n_gu, before)

        def dn_step(d, _):
            @pl.when(d + 3 < n_dn)
            def _():
                dn_copy(d + 3).start()

            @pl.when((d == 1) & (c == 0))
            def _():
                x_small(1).start()

            @pl.when((d == 1) & (c == 1))
            def _():
                x_big(0).start()

            @pl.when(d == 3)
            def _():
                for cp in gu_copies(0, lax.rem((c + 1) * n_gu, 2)):
                    cp.start()

            dn_copy(d).wait()

            @pl.when(d >= 1)
            def _():
                y_small(c, d - 1).wait()

            @pl.when((d >= 1) & (c == 0))
            def _():
                first_piece(d - 1).start()

            k = lax.rem(d, 4)
            at = pl.multiple_of(lax.rem(k, 2) * ND, ND)
            y = jnp.dot(g_v[0:M, :], wd_v[k // 2, :, pl.ds(at, ND)], preferred_element_type=f32)
            y_v[lax.rem(d, 2), 0:M, 0:ND] = y.astype(bf16)
            y_small(c, d).start()
            return 0

        lax.fori_loop(0, n_dn, dn_step, 0)
        y_small(c, n_dn - 1).wait()

        @pl.when(c == 0)
        def _():
            first_piece(n_dn - 1).start()

        @pl.when(c == 1)
        def _():
            copies[0].start()
        return 0

    n_big = TP - 1
    n_wide = D // BIG

    def big_chunk(c, _):
        x_big(c).wait()

        def before(j):
            @pl.when(j == n_gu - 2)
            def _():
                dn_big(0).start()

        gate_up(BIG, c * n_gu, before)

        def dn_step(d, _):
            @pl.when(d + 1 < n_wide)
            def _():
                dn_big(d + 1).start()

            @pl.when((d == 1) & (c + 1 < n_big))
            def _():
                x_big(c + 1).start()

            @pl.when((d == 2) & (c + 1 < n_big))
            def _():
                for cp in gu_copies(0, lax.rem((c + 1) * n_gu, 2)):
                    cp.start()

            dn_big(d).wait()

            @pl.when(d >= 1)
            def _():
                y_big(c, d - 1).wait()

            k = lax.rem(d, 2)
            for r in range(BIG // M):
                part = slice(r * M, (r + 1) * M)
                for q in range(BIG // ND):
                    cols = slice(q * ND, (q + 1) * ND)
                    y = jnp.dot(g_v[part, :], wd_v[k, :, cols], preferred_element_type=f32)
                    y_v[k, part, cols] = y.astype(bf16)
            y_big(c, d).start()
            return 0

        lax.fori_loop(0, n_wide, dn_step, 0)
        y_big(c, n_wide - 1).wait()

        @pl.when(c == 0)
        def _():
            for cp in copies[1:1 + TAIL]:
                cp.start()

        @pl.when(c == 1)
        def _():
            copies[1 + TAIL].start()
        return 0

    for cp in gu_copies(0, 0):
        cp.start()
    x_small(0).start()
    lax.fori_loop(0, 2, small_chunk, 0)
    lax.fori_loop(0, n_big, big_chunk, 0)
    for cp in [first_whole] + copies:
        cp.wait_recv()
    for cp in [first_whole] + copies:
        cp.wait_send()


def norm_kernel(res_ref, y_ref, r_ref, gain_ref, h_ref, n_ref):
    def rows_step(i, _):
        rows = pl.ds(pl.multiple_of(i * ROWS, ROWS), ROWS)
        y = y_ref[0, rows, :].astype(f32)
        for k in range(TP - 1):
            y = y + r_ref[k, rows, :].astype(f32)
        h = res_ref[rows, :].astype(f32) + y
        mean_sq = jnp.mean(h * h, axis=-1, keepdims=True)
        h_ref[rows, :] = h.astype(bf16)
        n_ref[rows, :] = (h * lax.rsqrt(mean_sq + EPS) * gain_ref[...]).astype(bf16)
        return 0

    lax.fori_loop(0, FB // ROWS, rows_step, 0, unroll=4)


def solution(mesh):
    def local_block(x_in, w_gate, w_up, w_down, residual, norm_gain):
        D, FS = w_gate.shape
        R = residual.shape[0]
        any_ = pl.BlockSpec(memory_space=pl.ANY)
        y, r = pl.pallas_call(
            matmul_kernel,
            out_shape=(jax.ShapeDtypeStruct((TP, R, D), bf16), jax.ShapeDtypeStruct((TP - 1, R, D), bf16)),
            in_specs=[any_] * 4,
            out_specs=(any_,) * 2,
            scratch_shapes=[
                pltpu.VMEM((BIG, D), bf16),
                pltpu.VMEM((2, D, 2 * SUB), bf16),
                pltpu.VMEM((2, D, 2 * SUB), bf16),
                pltpu.VMEM((2, FS, BIG), bf16),
                pltpu.VMEM((BIG, FS), bf16),
                pltpu.VMEM((2, BIG, BIG), bf16),
                pltpu.SemaphoreType.DMA,
                pltpu.SemaphoreType.DMA((2,)),
                pltpu.SemaphoreType.DMA((2,)),
                pltpu.SemaphoreType.DMA((4,)),
                pltpu.SemaphoreType.DMA((2,)),
                pltpu.SemaphoreType.DMA((3 + TAIL,)),
                pltpu.SemaphoreType.DMA((3 + TAIL,)),
            ],
            compiler_params=pltpu.CompilerParams(collective_id=0, has_side_effects=True, vmem_limit_bytes=60 * 1024 * 1024),
            name="mlp_matmuls",
        )(x_in, w_gate, w_up, w_down)
        row_block = pl.BlockSpec((FB, D), lambda b: (b, 0))
        return pl.pallas_call(
            norm_kernel,
            grid=(R // FB,),
            out_shape=(jax.ShapeDtypeStruct((R, D), bf16), jax.ShapeDtypeStruct((R, D), bf16)),
            in_specs=[row_block, pl.BlockSpec((1, FB, D), lambda b: (TP - 1, b, 0)),
                      pl.BlockSpec((TP - 1, FB, D), lambda b: (0, b, 0)), pl.BlockSpec((1, D), lambda b: (0, 0))],
            out_specs=(row_block, row_block),
            compiler_params=pltpu.CompilerParams(vmem_limit_bytes=48 * 1024 * 1024),
            name="sum_norm",
        )(residual, y, r, norm_gain.reshape(1, D))

    row_spec = P(("data", "tp"), None)
    return jax.shard_map(local_block, mesh=mesh, in_specs=(P("data", None), P(None, "tp"), P(None, "tp"), P("tp", None), row_spec, P(None)), out_specs=(row_spec, row_spec), check_vma=False)
```

time: 813 us -> 434 us (0.53)
  Pallas kernels: 0 us -> 434 us
  matrix products: 401 us -> 0 us
  blocking collectives: 382 us -> 0 us
  other arithmetic: 29.3 us -> 0 us
    pallas_call x0 -> x2, Pallas kernels: none -> 434 us  [the longest x1 412 us: local_block(): pl.pallas_call(matmul_kernel, out_shape=(jax.ShapeDtypeStruct((TP, R, D),...]
    dot_general x3 -> x0, matrix products: 401 us -> none  [the longest x1 135 us: local_block(): up_val = jnp.dot(x_in, w_up, preferred_element_type=jnp.float32)]
    all_to_all x1 -> x0, blocking collectives: 382 us -> none  [local_block(): received = lax.all_to_all(part_prod, 'tp', 0, 0, tiled=True)]
    reduce_sum x2 -> x0, other arithmetic: 21.5 us -> none  [the longest x1 19 us: local_block(): jnp.sum(received.reshape(tp_size, rows, received.shape[1]), axis=0, dtype...]
where the time goes in v2:
time: 434 us
  Pallas kernels  434 us (100%)
    pallas_call x1, Pallas kernels, local_block(): pl.pallas_call(matmul_kernel, out_shape=(jax.ShapeDtypeStruct((TP, R, D),...  412 us
    pallas_call x1, Pallas kernels, local_block(): pl.pallas_call(norm_kernel, grid=(R // FB,), out_shape=(jax.ShapeDtypeStr...  21.1 us

profile of v2, /device:TPU:0, one launch (start us, length us, event | category | flops | bytes accessed | tf_op | source)
XLA Modules:
  0.0 434.2 jit_solution(1475507810730961817)
XLA Ops:
  0.6 0.0 copy-start
  0.6 412.5 %mlp_matmuls.1 = (bf16[4,1024,4096]{2,1,0:T(8,128)(2,1)}, bf16[3,1024,4096]{2,1,0:T(8,128)(2,1)}) custom-call(bf16[4096,4096]{1,0:T(8,128)(2,1)} %x_hbm.1, bf16[4096,3584]{1,0:T(8,128)(2,1)} %wg_hbm.1, bf16[4096,3584]{1,0:T(8,128)(2,1)} %wu_hbm.1, bf16[3584,4096]{1,0:T(8,128)(2,1)} %wd_hbm.1), custom_call_target="tpu_custom_call" | custom-call | tf_op jit(solution)/shard_map/mlp_matmuls/pallas_call | solution.py:262
  413.1 0.0 copy-done
  413.1 21.1 %sum_norm.1 = (bf16[1024,4096]{1,0:T(8,128)(2,1)}, bf16[1024,4096]{1,0:T(8,128)(2,1)}) custom-call(bf16[1024,4096]{1,0:T(8,128)(2,1)} %res_ref.1, bf16[4,1024,4096]{2,1,0:T(8,128)(2,1)} %get-tuple-element.4.y_ref, bf16[3,1024,4096]{2,1,0:T(8,128)(2,1)} %get-tuple-element.5.r_ref, f32[1,4096]{1,0:T(1,128)S(1)} %bitcast.1), custom_call_target="tpu_custom_call" | custom-call | tf_op jit(solution)/shard_map/sum_norm/pallas_call | solution.py:286
Async XLA Ops:
  0.6 412.5 %copy-start = (f32[4096]{0:T(1024)S(1)}, f32[4096]{0:T(1024)}, u32[]{:S(2)}) copy-start(f32[4096]{0:T(1024)} %param.11) | copy-start | bytes 49156

commit v3 on v2

v3 whole, which is shorter than its diff:
```python
import jax
import jax.numpy as jnp
from jax import lax
from jax.experimental import pallas as pl
from jax.experimental.pallas import tpu as pltpu
from jax.sharding import PartitionSpec as P

EPS = 1e-5
TP = 4
SMALL = ((0, 384, 1), (384, 640, 2))
SUB = 256
ND = 512
BIG = 1024
TAIL = 4
FB = 256
ROWS = 8

bf16 = jnp.bfloat16
f32 = jnp.float32


def matmul_kernel(x_hbm, wg_hbm, wu_hbm, wd_hbm, res_hbm, y_hbm, r_hbm, hp_hbm,
                  x_v, wg_v, wu_v, wd_v, g_v, y_v, hp_v,
                  x_sem, wg_sem, wu_sem, wd_sem, y_sem, in_sem, hp_sem, send_sem, recv_sem):
    D, FS = wg_hbm.shape
    R = y_hbm.shape[1]
    assert R == BIG
    n_gu, n_dn = FS // (2 * SUB), D // ND
    me = lax.axis_index("tp")
    far_same = lax.rem(me + 2, TP)
    far_other = TP - 1 - me
    near = me + 1 - 2 * lax.rem(me, 2)
    peers = (far_same, far_other, near)

    def owner_of(c):
        own = c // 2
        mid = (1 - own) * ((1 - c) * far_other + c * near)
        return mid + own * me

    def x_small(c):
        first, m, _ = SMALL[c]
        row = pl.multiple_of(far_same * R + first, 128)
        return pltpu.make_async_copy(x_hbm.at[pl.ds(row, m), :], x_v.at[pl.ds(0, m), :], x_sem)

    def x_big(c):
        row = pl.multiple_of(owner_of(c) * R, BIG)
        return pltpu.make_async_copy(x_hbm.at[pl.ds(row, BIG), :], x_v, x_sem)

    def gu_copies(j, slot):
        col = pl.ds(pl.multiple_of(j * 2 * SUB, 2 * SUB), 2 * SUB)
        return (pltpu.make_async_copy(wg_hbm.at[:, col], wg_v.at[slot], wg_sem.at[slot]),
                pltpu.make_async_copy(wu_hbm.at[:, col], wu_v.at[slot], wu_sem.at[slot]))

    def dn_copy(d):
        k = lax.rem(d, 4)
        at = pl.ds(pl.multiple_of(lax.rem(k, 2) * ND, ND), ND)
        return pltpu.make_async_copy(wd_hbm.at[:, pl.ds(pl.multiple_of(d * ND, ND), ND)], wd_v.at[k // 2, :, at], wd_sem.at[k])

    def dn_big(d):
        k = lax.rem(d, 2)
        return pltpu.make_async_copy(wd_hbm.at[:, pl.ds(pl.multiple_of(d * BIG, BIG), BIG)], wd_v.at[k], wd_sem.at[k])

    def y_small(c, d):
        first, m, _ = SMALL[c]
        k = lax.rem(d, 2)
        return pltpu.make_async_copy(
            y_v.at[k, pl.ds(0, m), pl.ds(0, ND)],
            y_hbm.at[0, pl.ds(first, m), pl.ds(pl.multiple_of(d * ND, ND), ND)], y_sem.at[k])

    def y_big(c, d):
        k = lax.rem(d, 2)
        return pltpu.make_async_copy(y_v.at[k], y_hbm.at[c + 1, :, pl.ds(pl.multiple_of(d * BIG, BIG), BIG)], y_sem.at[k])

    def part_copies(d):
        k = lax.rem(d + 1, 2)
        out = []
        for q in range(2):
            cols = pl.ds(pl.multiple_of(d * BIG + q * ND, ND), ND)
            top, low = pl.ds(q * BIG, BIG), pl.ds((2 + q) * BIG, BIG)
            out.append(pltpu.make_async_copy(res_hbm.at[:, cols], wg_v.at[k, top, :], in_sem.at[k, 3 * q]))
            out.append(pltpu.make_async_copy(r_hbm.at[0, :, cols], wg_v.at[k, low, :], in_sem.at[k, 3 * q + 1]))
            out.append(pltpu.make_async_copy(r_hbm.at[2, :, cols], wu_v.at[k, top, :], in_sem.at[k, 3 * q + 2]))
        return out

    def hp_copies(d):
        return [pltpu.make_async_copy(hp_v.at[q], hp_hbm.at[:, pl.ds(pl.multiple_of(d * BIG + q * ND, ND), ND)], hp_sem.at[q])
                for q in range(2)]

    def remote(slot, row, rows, cols, ssem, rsem):
        ref = (slot, pl.ds(row, rows), slice(None) if cols is None else cols)
        return pltpu.make_async_remote_copy(
            src_ref=y_hbm.at[ref], dst_ref=r_hbm.at[ref], send_sem=ssem, recv_sem=rsem,
            device_id={"tp": peers[slot]}, device_id_type=pl.DeviceIdType.MESH)

    def small_piece(c, d):
        first, m, _ = SMALL[c]
        return remote(0, first, m, pl.ds(pl.multiple_of(d * ND, ND), ND), send_sem.at[c], recv_sem.at[c])

    small_whole = [remote(0, first, m, None, send_sem.at[c], recv_sem.at[c]) for c, (first, m, _) in enumerate(SMALL)]
    rows = R // TAIL
    far_copies = [remote(1, t * rows, rows, None, send_sem.at[2 + t], recv_sem.at[2 + t]) for t in range(TAIL)]
    near_copy = remote(2, 0, R, None, send_sem.at[2 + TAIL], recv_sem.at[2 + TAIL])

    def row_parts(m, n):
        return [slice(r * (m // n), (r + 1) * (m // n)) for r in range(n)]

    def hidden(parts, slot, j):
        for q in range(2):
            cols = slice(q * SUB, (q + 1) * SUB)
            for part in parts:
                gate = jnp.dot(x_v[part, :], wg_v[slot, :, cols], preferred_element_type=f32)
                up = jnp.dot(x_v[part, :], wu_v[slot, :, cols], preferred_element_type=f32)
                g_v[part, pl.ds(pl.multiple_of(j * 2 * SUB + q * SUB, SUB), SUB)] = (gate * jax.nn.sigmoid(gate) * up).astype(bf16)

    def gate_up(parts, base, before):
        def gu_step(j, _):
            slot = lax.rem(base + j, 2)

            @pl.when(j + 1 < n_gu)
            def _():
                for cp in gu_copies(j + 1, 1 - slot):
                    cp.start()

            before(j)
            for cp in gu_copies(j, slot):
                cp.wait()
            hidden(parts, slot, j)
            return 0

        lax.fori_loop(0, n_gu, gu_step, 0)

    def small_chunk(c):
        _, m, n = SMALL[c]
        parts = row_parts(m, n)
        x_small(c).wait()

        def before(j):
            @pl.when(j >= n_gu - 3)
            def _():
                dn_copy(j - (n_gu - 3)).start()

        gate_up(parts, c * n_gu, before)

        def dn_step(d, _):
            @pl.when(d + 3 < n_dn)
            def _():
                dn_copy(d + 3).start()

            @pl.when(d == 1)
            def _():
                (x_small(1) if c == 0 else x_big(0)).start()

            @pl.when(d == 3)
            def _():
                for cp in gu_copies(0, (c + 1) * n_gu % 2):
                    cp.start()

            dn_copy(d).wait()

            @pl.when(d >= 1)
            def _():
                y_small(c, d - 1).wait()
                small_piece(c, d - 1).start()

            k = lax.rem(d, 4)
            at = pl.multiple_of(lax.rem(k, 2) * ND, ND)
            for part in parts:
                y = jnp.dot(g_v[part, :], wd_v[k // 2, :, pl.ds(at, ND)], preferred_element_type=f32)
                y_v[lax.rem(d, 2), part, 0:ND] = y.astype(bf16)
            y_small(c, d).start()
            return 0

        lax.fori_loop(0, n_dn, dn_step, 0)
        y_small(c, n_dn - 1).wait()
        small_piece(c, n_dn - 1).start()

    n_big = TP - 1
    n_wide = D // BIG

    def big_chunk(c, _):
        x_big(c).wait()

        def before(j):
            @pl.when(j == n_gu - 2)
            def _():
                dn_big(0).start()

            @pl.when((c == n_big - 1) & (j == n_gu - 1))
            def _():
                for cp in (*small_whole, near_copy):
                    cp.wait_recv()
                for cp in part_copies(0):
                    cp.start()

        gate_up(row_parts(BIG, 2), c * n_gu, before)

        def dn_step(d, _):
            @pl.when(d + 1 < n_wide)
            def _():
                dn_big(d + 1).start()

            @pl.when(d == 1)
            def _():
                x_big(c + 1).start()

            @pl.when(d == 2)
            def _():
                for cp in gu_copies(0, lax.rem((c + 1) * n_gu, 2)):
                    cp.start()

            dn_big(d).wait()

            @pl.when(d >= 1)
            def _():
                y_big(c, d - 1).wait()

            k = lax.rem(d, 2)
            for part in row_parts(BIG, 2):
                for q in range(BIG // ND):
                    cols = slice(q * ND, (q + 1) * ND)
                    y = jnp.dot(g_v[part, :], wd_v[k, :, cols], preferred_element_type=f32)
                    y_v[k, part, cols] = y.astype(bf16)
            y_big(c, d).start()
            return 0

        def own_step(d, _):
            @pl.when(d + 1 < n_wide)
            def _():
                dn_big(d + 1).start()
                for cp in part_copies(d + 1):
                    cp.start()

            dn_big(d).wait()
            for cp in part_copies(d):
                cp.wait()

            @pl.when(d >= 1)
            def _():
                for cp in hp_copies(d - 1):
                    cp.wait()

            k, t = lax.rem(d, 2), lax.rem(d + 1, 2)
            for part in row_parts(BIG, 2):
                for q in range(2):
                    cols = slice(q * ND, (q + 1) * ND)
                    at = slice(q * BIG + part.start, q * BIG + part.stop)
                    low = slice((2 + q) * BIG + part.start, (2 + q) * BIG + part.stop)
                    y = jnp.dot(g_v[part, :], wd_v[k, :, cols], preferred_element_type=f32).astype(bf16).astype(f32)
                    y = y + wg_v[t, low, :].astype(f32) + wu_v[t, at, :].astype(f32)
                    hp_v[q, part, :] = wg_v[t, at, :].astype(f32) + y
            for cp in hp_copies(d):
                cp.start()
            return 0

        @pl.when(c + 1 < n_big)
        def _():
            lax.fori_loop(0, n_wide, dn_step, 0)
            y_big(c, n_wide - 1).wait()

        @pl.when(c + 1 == n_big)
        def _():
            lax.fori_loop(0, n_wide, own_step, 0)
            for cp in hp_copies(n_wide - 1):
                cp.wait()

        @pl.when(c == 0)
        def _():
            for cp in far_copies:
                cp.start()

        @pl.when(c == 1)
        def _():
            near_copy.start()
        return 0

    for cp in gu_copies(0, 0):
        cp.start()
    x_small(0).start()
    barrier = pltpu.get_barrier_semaphore()
    for peer in peers:
        pl.semaphore_signal(barrier, inc=1, device_id={"tp": peer}, device_id_type=pl.DeviceIdType.MESH)
    pl.semaphore_wait(barrier, TP - 1)

    small_chunk(0)
    small_chunk(1)
    lax.fori_loop(0, n_big, big_chunk, 0)
    for cp in far_copies:
        cp.wait_recv()
    for cp in (*small_whole, *far_copies, near_copy):
        cp.wait_send()


def norm_kernel(hp_ref, r_ref, gain_ref, h_ref, n_ref):
    def rows_step(i, _):
        rows = pl.ds(pl.multiple_of(i * ROWS, ROWS), ROWS)
        h = hp_ref[rows, :] + r_ref[0, rows, :].astype(f32)
        mean_sq = jnp.mean(h * h, axis=-1, keepdims=True)
        h_ref[rows, :] = h.astype(bf16)
        n_ref[rows, :] = (h * lax.rsqrt(mean_sq + EPS) * gain_ref[...]).astype(bf16)
        return 0

    lax.fori_loop(0, FB // ROWS, rows_step, 0, unroll=4)


def solution(mesh):
    def local_block(x_in, w_gate, w_up, w_down, residual, norm_gain):
        D, FS = w_gate.shape
        R = residual.shape[0]
        any_ = pl.BlockSpec(memory_space=pl.ANY)
        _, r, hp = pl.pallas_call(
            matmul_kernel,
            out_shape=(jax.ShapeDtypeStruct((TP - 1, R, D), bf16), jax.ShapeDtypeStruct((TP - 1, R, D), bf16), jax.ShapeDtypeStruct((R, D), f32)),
            in_specs=[any_] * 5,
            out_specs=(any_,) * 3,
            scratch_shapes=[
                pltpu.VMEM((BIG, D), bf16),
                pltpu.VMEM((2, D, 2 * SUB), bf16),
                pltpu.VMEM((2, D, 2 * SUB), bf16),
                pltpu.VMEM((2, FS, BIG), bf16),
                pltpu.VMEM((BIG, FS), bf16),
                pltpu.VMEM((2, BIG, BIG), bf16),
                pltpu.VMEM((2, BIG, ND), f32),
                pltpu.SemaphoreType.DMA,
                pltpu.SemaphoreType.DMA((2,)),
                pltpu.SemaphoreType.DMA((2,)),
                pltpu.SemaphoreType.DMA((4,)),
                pltpu.SemaphoreType.DMA((2,)),
                pltpu.SemaphoreType.DMA((2, 6)),
                pltpu.SemaphoreType.DMA((2,)),
                pltpu.SemaphoreType.DMA((3 + TAIL,)),
                pltpu.SemaphoreType.DMA((3 + TAIL,)),
            ],
            compiler_params=pltpu.CompilerParams(collective_id=0, has_side_effects=True, vmem_limit_bytes=60 * 1024 * 1024),
            name="mlp_matmuls",
        )(x_in, w_gate, w_up, w_down, residual)
        row_block = pl.BlockSpec((FB, D), lambda b: (b, 0))
        return pl.pallas_call(
            norm_kernel,
            grid=(R // FB,),
            out_shape=(jax.ShapeDtypeStruct((R, D), bf16), jax.ShapeDtypeStruct((R, D), bf16)),
            in_specs=[row_block, pl.BlockSpec((1, FB, D), lambda b: (1, b, 0)), pl.BlockSpec((1, D), lambda b: (0, 0))],
            out_specs=(row_block, row_block),
            compiler_params=pltpu.CompilerParams(vmem_limit_bytes=48 * 1024 * 1024),
            name="sum_norm",
        )(hp, r, norm_gain.reshape(1, D))

    row_spec = P(("data", "tp"), None)
    return jax.shard_map(local_block, mesh=mesh, in_specs=(P("data", None), P(None, "tp"), P(None, "tp"), P("tp", None), row_spec, P(None)), out_specs=(row_spec, row_spec), check_vma=False)
```

time: 434 us -> 431 us (level)
    pallas_call x1, Pallas kernels: 21.1 us -> 15.3 us  [local_block(): pl.pallas_call(norm_kernel, grid=(R // FB,), out_shape=(jax.ShapeDtypeStr...]
where the time goes in v3:
time: 431 us; the launch traced here: 430 us
  Pallas kernels  430 us (100%)
    pallas_call x1, Pallas kernels, local_block(): pl.pallas_call(matmul_kernel, out_shape=(jax.ShapeDtypeStruct((TP - 1, R,...  414 us
    pallas_call x1, Pallas kernels, local_block(): pl.pallas_call(norm_kernel, grid=(R // FB,), out_shape=(jax.ShapeDtypeStr...  15.3 us

profile of v3, /device:TPU:0, one launch (start us, length us, event | category | flops | bytes accessed | tf_op | source)
XLA Modules:
  0.0 430.4 jit_solution(407308332493615675)
XLA Ops:
  0.6 0.0 copy-start
  0.6 414.5 %mlp_matmuls.1 = (bf16[3,1024,4096]{2,1,0:T(8,128)(2,1)}, bf16[3,1024,4096]{2,1,0:T(8,128)(2,1)}, f32[1024,4096]{1,0:T(8,128)}) custom-call(bf16[4096,4096]{1,0:T(8,128)(2,1)} %x_hbm.1, bf16[4096,3584]{1,0:T(8,128)(2,1)} %wg_hbm.1, bf16[4096,3584]{1,0:T(8,128)(2,1)} %wu_hbm.1, bf16[3584,4096]{1,0:T(8,128)(2,1)} %wd_hbm.1, bf16[1024,4096]{1,0:T(8,128)(2,1)} %res_hbm.1), custom_call_target="tpu_custom_call" | custom-call | tf_op jit(solution)/shard_map/mlp_matmuls/pallas_call | solution.py:310
  415.1 0.0 copy-done
  415.1 15.3 %sum_norm.1 = (bf16[1024,4096]{1,0:T(8,128)(2,1)}, bf16[1024,4096]{1,0:T(8,128)(2,1)}) custom-call(f32[1024,4096]{1,0:T(8,128)} %get-tuple-element.4.hp_ref, bf16[3,1024,4096]{2,1,0:T(8,128)(2,1)} %get-tuple-element.5.r_ref, f32[1,4096]{1,0:T(1,128)S(1)} %bitcast.1), custom_call_target="tpu_custom_call" | custom-call | tf_op jit(solution)/shard_map/sum_norm/pallas_call | solution.py:337
Async XLA Ops:
  0.6 414.5 %copy-start = (f32[4096]{0:T(1024)S(1)}, f32[4096]{0:T(1024)}, u32[]{:S(2)}) copy-start(f32[4096]{0:T(1024)} %param.11) | copy-start | bytes 49156

commit v4 on v3

--- a/solution.py
+++ b/solution.py
@@ -25,7 +25,7 @@
     D, FS = wg_hbm.shape
     R = y_hbm.shape[1]
     assert R == BIG
-    n_gu, n_dn = FS // (2 * SUB), D // ND
+    n_gu = FS // (2 * SUB)
     me = lax.axis_index("tp")
     far_same = lax.rem(me + 2, TP)
     far_other = TP - 1 - me
@@ -51,11 +51,6 @@
         return (pltpu.make_async_copy(wg_hbm.at[:, col], wg_v.at[slot], wg_sem.at[slot]),
                 pltpu.make_async_copy(wu_hbm.at[:, col], wu_v.at[slot], wu_sem.at[slot]))
 
-    def dn_copy(d):
-        k = lax.rem(d, 4)
-        at = pl.ds(pl.multiple_of(lax.rem(k, 2) * ND, ND), ND)
-        return pltpu.make_async_copy(wd_hbm.at[:, pl.ds(pl.multiple_of(d * ND, ND), ND)], wd_v.at[k // 2, :, at], wd_sem.at[k])
-
     def dn_big(d):
         k = lax.rem(d, 2)
         return pltpu.make_async_copy(wd_hbm.at[:, pl.ds(pl.multiple_of(d * BIG, BIG), BIG)], wd_v.at[k], wd_sem.at[k])
@@ -64,8 +59,8 @@
         first, m, _ = SMALL[c]
         k = lax.rem(d, 2)
         return pltpu.make_async_copy(
-            y_v.at[k, pl.ds(0, m), pl.ds(0, ND)],
-            y_hbm.at[0, pl.ds(first, m), pl.ds(pl.multiple_of(d * ND, ND), ND)], y_sem.at[k])
+            y_v.at[k, pl.ds(0, m), pl.ds(0, BIG)],
+            y_hbm.at[0, pl.ds(first, m), pl.ds(pl.multiple_of(d * BIG, BIG), BIG)], y_sem.at[k])
 
     def y_big(c, d):
         k = lax.rem(d, 2)
@@ -94,7 +89,7 @@
 
     def small_piece(c, d):
         first, m, _ = SMALL[c]
-        return remote(0, first, m, pl.ds(pl.multiple_of(d * ND, ND), ND), send_sem.at[c], recv_sem.at[c])
+        return remote(0, first, m, pl.ds(pl.multiple_of(d * BIG, BIG), BIG), send_sem.at[c], recv_sem.at[c])
 
     small_whole = [remote(0, first, m, None, send_sem.at[c], recv_sem.at[c]) for c, (first, m, _) in enumerate(SMALL)]
     rows = R // TAIL
@@ -129,53 +124,55 @@
 
         lax.fori_loop(0, n_gu, gu_step, 0)
 
+    n_wide = D // BIG
+
     def small_chunk(c):
         _, m, n = SMALL[c]
         parts = row_parts(m, n)
         x_small(c).wait()
 
         def before(j):
-            @pl.when(j >= n_gu - 3)
-            def _():
-                dn_copy(j - (n_gu - 3)).start()
+            @pl.when(j == n_gu - 2)
+            def _():
+                dn_big(0).start()
 
         gate_up(parts, c * n_gu, before)
 
         def dn_step(d, _):
-            @pl.when(d + 3 < n_dn)
-            def _():
-                dn_copy(d + 3).start()
+            @pl.when(d + 1 < n_wide)
+            def _():
+                dn_big(d + 1).start()
 
             @pl.when(d == 1)
             def _():
                 (x_small(1) if c == 0 else x_big(0)).start()
 
-            @pl.when(d == 3)
+            @pl.when(d == 2)
             def _():
                 for cp in gu_copies(0, (c + 1) * n_gu % 2):
                     cp.start()
 
-            dn_copy(d).wait()
+            dn_big(d).wait()
 
             @pl.when(d >= 1)
             def _():
                 y_small(c, d - 1).wait()
                 small_piece(c, d - 1).start()
 
-            k = lax.rem(d, 4)
-            at = pl.multiple_of(lax.rem(k, 2) * ND, ND)
+            k = lax.rem(d, 2)
             for part in parts:
-                y = jnp.dot(g_v[part, :], wd_v[k // 2, :, pl.ds(at, ND)], preferred_element_type=f32)
-                y_v[lax.rem(d, 2), part, 0:ND] = y.astype(bf16)
+                for q in range(BIG // SUB):
+                    cols = slice(q * SUB, (q + 1) * SUB)
+                    y = jnp.dot(g_v[part, :], wd_v[k, :, cols], preferred_element_type=f32)
+                    y_v[k, part, cols] = y.astype(bf16)
             y_small(c, d).start()
             return 0
 
-        lax.fori_loop(0, n_dn, dn_step, 0)
-        y_small(c, n_dn - 1).wait()
-        small_piece(c, n_dn - 1).start()
+        lax.fori_loop(0, n_wide, dn_step, 0)
+        y_small(c, n_wide - 1).wait()
+        small_piece(c, n_wide - 1).start()
 
     n_big = TP - 1
-    n_wide = D // BIG
 
     def big_chunk(c, _):
         x_big(c).wait()
@@ -216,8 +213,8 @@
 
             k = lax.rem(d, 2)
             for part in row_parts(BIG, 2):
-                for q in range(BIG // ND):
-                    cols = slice(q * ND, (q + 1) * ND)
+                for q in range(BIG // SUB):
+                    cols = slice(q * SUB, (q + 1) * SUB)
                     y = jnp.dot(g_v[part, :], wd_v[k, :, cols], preferred_element_type=f32)
                     y_v[k, part, cols] = y.astype(bf16)
             y_big(c, d).start()
@@ -241,13 +238,14 @@
 
             k, t = lax.rem(d, 2), lax.rem(d + 1, 2)
             for part in row_parts(BIG, 2):
-                for q in range(2):
-                    cols = slice(q * ND, (q + 1) * ND)
+                for q, u in ((0, 0), (0, 1), (1, 0), (1, 1)):
+                    cols = slice(q * ND + u * SUB, q * ND + (u + 1) * SUB)
+                    sub = slice(u * SUB, (u + 1) * SUB)
                     at = slice(q * BIG + part.start, q * BIG + part.stop)
                     low = slice((2 + q) * BIG + part.start, (2 + q) * BIG + part.stop)
                     y = jnp.dot(g_v[part, :], wd_v[k, :, cols], preferred_element_type=f32).astype(bf16).astype(f32)
-                    y = y + wg_v[t, low, :].astype(f32) + wu_v[t, at, :].astype(f32)
-                    hp_v[q, part, :] = wg_v[t, at, :].astype(f32) + y
+                    y = y + wg_v[t, low, sub].astype(f32) + wu_v[t, at, sub].astype(f32)
+                    hp_v[q, part, sub] = wg_v[t, at, sub].astype(f32) + y
             for cp in hp_copies(d):
                 cp.start()
             return 0
@@ -323,7 +321,7 @@
                 pltpu.SemaphoreType.DMA,
                 pltpu.SemaphoreType.DMA((2,)),
                 pltpu.SemaphoreType.DMA((2,)),
-                pltpu.SemaphoreType.DMA((4,)),
+                pltpu.SemaphoreType.DMA((2,)),
                 pltpu.SemaphoreType.DMA((2,)),
                 pltpu.SemaphoreType.DMA((2, 6)),
                 pltpu.SemaphoreType.DMA((2,)),

time: 431 us -> 423 us (0.981)
  Pallas kernels: 430 us -> 423 us
    pallas_call x1, Pallas kernels: 414 us -> 407 us  [local_block(): pl.pallas_call(matmul_kernel, out_shape=(jax.ShapeDtypeStruct((TP - 1, R,...]
where the time goes in v4:
time: 423 us
  Pallas kernels  423 us (100%)
    pallas_call x1, Pallas kernels, local_block(): pl.pallas_call(matmul_kernel, out_shape=(jax.ShapeDtypeStruct((TP - 1, R,...  407 us
    pallas_call x1, Pallas kernels, local_block(): pl.pallas_call(norm_kernel, grid=(R // FB,), out_shape=(jax.ShapeDtypeStr...  15.3 us

profile of v4, /device:TPU:0, one launch (start us, length us, event | category | flops | bytes accessed | tf_op | source)
XLA Modules:
  0.0 423.2 jit_solution(9488675231181461799)
XLA Ops:
  0.6 0.0 copy-start
  0.6 407.3 %mlp_matmuls.1 = (bf16[3,1024,4096]{2,1,0:T(8,128)(2,1)}, bf16[3,1024,4096]{2,1,0:T(8,128)(2,1)}, f32[1024,4096]{1,0:T(8,128)}) custom-call(bf16[4096,4096]{1,0:T(8,128)(2,1)} %x_hbm.1, bf16[4096,3584]{1,0:T(8,128)(2,1)} %wg_hbm.1, bf16[4096,3584]{1,0:T(8,128)(2,1)} %wu_hbm.1, bf16[3584,4096]{1,0:T(8,128)(2,1)} %wd_hbm.1, bf16[1024,4096]{1,0:T(8,128)(2,1)} %res_hbm.1), custom_call_target="tpu_custom_call" | custom-call | tf_op jit(solution)/shard_map/mlp_matmuls/pallas_call | solution.py:308
  408.0 0.0 copy-done
  408.0 15.3 %sum_norm.1 = (bf16[1024,4096]{1,0:T(8,128)(2,1)}, bf16[1024,4096]{1,0:T(8,128)(2,1)}) custom-call(f32[1024,4096]{1,0:T(8,128)} %get-tuple-element.4.hp_ref, bf16[3,1024,4096]{2,1,0:T(8,128)(2,1)} %get-tuple-element.5.r_ref, f32[1,4096]{1,0:T(1,128)S(1)} %bitcast.1), custom_call_target="tpu_custom_call" | custom-call | tf_op jit(solution)/shard_map/sum_norm/pallas_call | solution.py:335
Async XLA Ops:
  0.6 407.3 %copy-start = (f32[4096]{0:T(1024)S(1)}, f32[4096]{0:T(1024)}, u32[]{:S(2)}) copy-start(f32[4096]{0:T(1024)} %param.11) | copy-start | bytes 49156
